TPU v7x, 256 devices: a whole 4x4x8 slice. The times are simulated.
256 devices in a mesh: dp: 16 (over y, x_hi, core), tensor: 16 (over x_lo, z).
Axes of the slice: x: 4 (x_hi: 2, x_lo: 2; x = x_hi * 2 + x_lo), y: 4, z: 8, core: 2. Of those that a mesh axis runs over, the one named last changes fastest.
Arguments:
- h_values: bfloat16 [12288, 16384], P(('dp', 'tensor')), may hold values from -448 to 448
- h_scales: bfloat16 [12288, 128], P(('dp', 'tensor')), may hold values from 0.00049972534 to 0.0099487305
- dy_values: bfloat16 [12288, 4096], P(('dp', 'tensor')), may hold values from -448 to 448
- dy_scales: bfloat16 [12288, 32], P(('dp', 'tensor')), may hold values from 1.9907951e-05 to 0.00039863586
Outputs:
- grad_down: bfloat16 [4096, 16384], P('dp', 'tensor')
All inputs are finite; a program needn't handle non-finite values.
Results may differ from a plain program's by a relative error of at most 0.02.
Values may be sent and summed in bfloat16 or wider, within the bound.
A program may use at most 192 MiB of HBM per device.

v0:
```python
import jax
import jax.numpy as jnp
from jax import lax
from jax.sharding import PartitionSpec as P

QBLOCK = 128


def dequantize(values, scales):
    row_count, col_count = values.shape
    block_total = scales.shape[1]
    widened = values.astype(jnp.float32).reshape(row_count, block_total, col_count // block_total)
    widened = widened * scales.astype(jnp.float32)[:, :, None]
    return widened.reshape(row_count, col_count)


def requantize(field):
    row_count, col_count = field.shape
    blocked = field.reshape(row_count // QBLOCK, QBLOCK, col_count)
    largest = jnp.max(jnp.abs(blocked), axis=1)
    column_scale = ((largest + 1e-06) / 448.0).astype(jnp.bfloat16)
    quantized = (blocked / column_scale.astype(jnp.float32)[:, None, :]).astype(jnp.bfloat16)
    return (quantized.reshape(row_count, col_count), column_scale)


def group_product(grad_q, grad_scale, hidden_q, hidden_scale):
    block_count = grad_q.shape[0] // QBLOCK
    summed = jnp.zeros((grad_q.shape[1], hidden_q.shape[1]), jnp.float32)
    for block_index in range(block_count):
        grad_block = grad_q[block_index * QBLOCK : (block_index + 1) * QBLOCK]
        hidden_block = hidden_q[block_index * QBLOCK : (block_index + 1) * QBLOCK]
        product = lax.dot_general(
            grad_block, hidden_block, (((0,), (0,)), ((), ())), preferred_element_type=jnp.float32
        )
        row_factor = grad_scale[block_index].astype(jnp.float32)[:, None]
        col_factor = hidden_scale[block_index].astype(jnp.float32)[None, :]
        summed = summed + product * row_factor * col_factor
    return summed


def shards(h_values, h_scales, dy_values, dy_scales):
    hidden_vals, hidden_blocks = (
        lax.all_to_all(h_values, "tensor", split_axis=1, concat_axis=0, tiled=True),
        lax.all_to_all(h_scales, "tensor", split_axis=1, concat_axis=0, tiled=True),
    )
    grad_vals, grad_blocks = (
        lax.all_gather(dy_values, "tensor", axis=0, tiled=True),
        lax.all_gather(dy_scales, "tensor", axis=0, tiled=True),
    )
    hidden_q, hidden_scale = requantize(dequantize(hidden_vals, hidden_blocks))
    grad_q, grad_scale = requantize(dequantize(grad_vals, grad_blocks))
    return lax.psum_scatter(
        group_product(grad_q, grad_scale, hidden_q, hidden_scale).astype(jnp.bfloat16),
        "dp",
        scatter_dimension=0,
        tiled=True,
    )


def solution(mesh):
    placed = (
        P(("dp", "tensor"), None),
        P(("dp", "tensor"), None),
        P(("dp", "tensor"), None),
        P(("dp", "tensor"), None),
    )
    return jax.shard_map(
        shards, mesh=mesh, in_specs=placed, out_specs=P("dp", "tensor"), check_vma=False
    )
```

profile of v0, /device:TPU:8, one launch (start us, length us, event | category | flops | bytes accessed | tf_op | source)
XLA Modules:
  0.0 344.4 jit_solution(2101893840816630577)
XLA Ops:
  6.5 0.0 all-gather.3.cloned.1.call-start
  6.5 0.7 all-gather.3.cloned.1.call-update
  7.3 0.8 copy.19
  8.1 0.7 reshape.117
  8.8 9.5 %all-to-all-start.1 = ((bf16[16,2,192]{2,1,0:T(2,128)(2,1)}), bf16[16,2,192]{2,1,0:T(2,128)(2,1)S(1)}, u32[]{:S(2)}, u32[]{:S(2)}) async-start(bf16[16,2,192]{2,1,0:T(2,128)(2,1)} %reshape.117), calls=%async_computation.1 | async-start | bytes 32768 | tf_op jit(solution)/shard_map/all_to_all | solution.py:44
  18.3 2.7 copy.28
  21.0 5.8 %all-to-all-done.1 = bf16[16,2,192]{2,1,0:T(2,128)(2,1)S(1)} async-done(((bf16[16,2,192]{2,1,0:T(2,128)(2,1)}), bf16[16,2,192]{2,1,0:T(2,128)(2,1)S(1)}, u32[]{:S(2)}, u32[]{:S(2)}) %all-to-all-start.1) | async-done | bytes 12320 | tf_op jit(solution)/shard_map/all_to_all | solution.py:44
  26.8 4.4 %all-to-all-start = ((bf16[48,16,1024]{2,0,1:T(8,128)(2,1)}), bf16[48,16,1024]{2,0,1:T(8,128)(2,1)}, u32[]{:S(2)}, u32[]{:S(2)}) async-start(bf16[48,16,1024]{2,0,1:T(8,128)(2,1)} %bitcast.67), calls=%async_computation | async-start | bytes 3145728 | tf_op jit(solution)/shard_map/all_to_all | solution.py:43
  31.2 0.0 reduce-scatter.2.cloned.1.call-start
  31.3 82.0 %all-gather = bf16[16,48,32]{1,2,0:T(8,128)(2,1)S(1)} all-gather(bf16[1,48,32]{1,2,0:T(8,128)(2,1)} %bitcast.80), channel_id=1, replica_groups=mesh['dp'=16,'tensor'=16] {'tensor'}, dimensions={0}, use_global_device_ids=true | all-gather | bytes 52224 | tf_op jit(solution)/shard_map/all_gather | solution.py:48
  113.3 0.1 copy.22
  113.4 7.1 %mul.148 = f32[768,32,128]{2,1,0:T(8,128)} broadcast(f32[768,32]{1,0:T(8,128)S(1)} %bitcast.71), dimensions={0,1} | broadcast | bytes 12681216 | tf_op jit(solution)/shard_map/mul | solution.py:13
  120.5 13.8 %mul.149 = f32[6,128,4096]{2,1,0:T(8,128)} reshape(f32[768,32,128]{2,1,0:T(8,128)} %mul.148) | data formatting | bytes 25165824 | tf_op jit(solution)/shard_map/mul | solution.py:13
  134.3 0.1 reshape.118
  134.4 0.2 copy.23
  134.6 0.9 mul.151
  135.4 2.4 mul.152
  137.8 0.0 all-to-all-done
  137.8 1.8 convert_element_type.171
  139.6 2.6 abs_reduce_fusion.1
  142.3 0.5 divide_convert_fusion.1
  142.8 0.0 all-gather.3.cloned.1.call-done
  142.8 8.5 %abs_reduce_fusion = f32[6,4096]{1,0:T(8,128)S(1)} fusion(f32[6,128,4096]{2,1,0:T(8,128)} %mul.149, bf16[6,128,4096]{2,1,0:T(8,128)(2,1)} %bitcast.68), kind=kLoop, calls=%fused_computation.3 | loop fusion | flops 12558336 | bytes 18972672 | tf_op jit(solution)/shard_map/reduce_max | solution.py:20
  151.3 7.6 %divide_convert_fusion = bf16[6,128,4096]{2,1,0:T(8,128)(2,1)S(1)} fusion(f32[6,128,4096]{2,1,0:T(8,128)} %mul.149, bf16[6,128,4096]{2,1,0:T(8,128)(2,1)} %bitcast.69, f32[6,4096]{1,0:T(8,128)S(1)} %get-tuple-element.9), kind=kLoop, calls=%fused_computation.2 | loop fusion | flops 12582912 | bytes 25264128 | tf_op jit(solution)/shard_map/convert_element_type | solution.py:22
  158.9 0.0 copy-start
  158.9 8.1 %fusion = f32[4096,1024]{1,0:T(8,128)} fusion(bf16[6,128,4096]{2,1,0:T(8,128)(2,1)S(1)} %divide_convert_fusion, bf16[6,128,1024]{2,1,0:T(8,128)(2,1)S(1)} %divide_convert_fusion.1), kind=kOutput, calls=%fused_computation.9 | convolution fusion | flops 1073741824 | bytes 18087936 | tf_op jit(solution)/shard_map/dot_general | solution.py:32
  167.0 8.1 %fusion.1 = f32[4096,1024]{1,0:T(8,128)} fusion(bf16[6,128,4096]{2,1,0:T(8,128)(2,1)S(1)} %divide_convert_fusion, bf16[6,128,1024]{2,1,0:T(8,128)(2,1)S(1)} %divide_convert_fusion.1), kind=kOutput, calls=%fused_computation.11 | convolution fusion | flops 1073741824 | bytes 18087936 | tf_op jit(solution)/shard_map/dot_general | solution.py:32
  175.1 8.1 %fusion.2 = f32[4096,1024]{1,0:T(8,128)} fusion(bf16[6,128,4096]{2,1,0:T(8,128)(2,1)S(1)} %divide_convert_fusion, bf16[6,128,1024]{2,1,0:T(8,128)(2,1)S(1)} %divide_convert_fusion.1), kind=kOutput, calls=%fused_computation.13 | convolution fusion | flops 1073741824 | bytes 18087936 | tf_op jit(solution)/shard_map/dot_general | solution.py:32
  183.2 8.1 %fusion.3 = f32[4096,1024]{1,0:T(8,128)} fusion(bf16[6,128,4096]{2,1,0:T(8,128)(2,1)S(1)} %divide_convert_fusion, bf16[6,128,1024]{2,1,0:T(8,128)(2,1)S(1)} %divide_convert_fusion.1), kind=kOutput, calls=%fused_computation.15 | convolution fusion | flops 1073741824 | bytes 18087936 | tf_op jit(solution)/shard_map/dot_general | solution.py:32
  191.3 0.0 copy-done
  191.3 8.2 %fusion.4 = f32[4096,1024]{1,0:T(8,128)} fusion(bf16[6,128,4096]{2,1,0:T(8,128)(2,1)S(1)} %divide_convert_fusion, bf16[6,128,1024]{2,1,0:T(8,128)(2,1)S(1)} %divide_convert_fusion.1), kind=kOutput, calls=%fused_computation.17 | convolution fusion | flops 1073741824 | bytes 18087936 | tf_op jit(solution)/shard_map/dot_general | solution.py:32
  199.5 0.1 slice_convert_fusion.5
  199.6 32.2 %add_convert_fusion = bf16[4096,1024]{1,0:T(8,128)(2,1)} fusion(f32[4096,1024]{1,0:T(8,128)} %fusion, f32[4096,1024]{1,0:T(8,128)} %fusion.1, f32[4096,1024]{1,0:T(8,128)} %fusion.2, f32[4096,1024]{1,0:T(8,128)} %fusion.3, f32[4096,1024]{1,0:T(8,128)} %fusion.4, f32[1024]{0:T(1024)S(1)} %bitcast.86, f32[4096]{0:T(1024)S(1)} %bitcast.79, ...), kind=kOutput, calls=%fused_computation | convolution fusion | flops 1149239296 | bytes 93708288 | tf_op jit(solution)/shard_map/dot_general | solution.py:32
  231.8 0.0 reduce-scatter.2.cloned.1.call-update
  231.8 105.8 %reduce-scatter.2.cloned.1.call-done = bf16[256,1024]{1,0:T(8,128)(2,1)} async-done(((bf16[4096,1024]{1,0:T(8,128)(2,1)}), bf16[256,1024]{1,0:T(8,128)(2,1)}) %reduce-scatter.2.cloned.1.call-update) | async-done | bytes 524304 | tf_op jit(solution)/shard_map/reduce_scatter | solution.py:52
  (5 shorter events, 0.1 us)
Async XLA Ops:
  6.5 136.3 %all-gather.3.cloned.1.call-start = ((), (), s32[]{:S(2)}) async-start(), calls=%async_computation.3 | async-start | bytes 6684672 | tf_op jit(solution)/shard_map/all_gather | solution.py:47
  8.8 18.0 %all-to-all-start.1 = ((bf16[16,2,192]{2,1,0:T(2,128)(2,1)}), bf16[16,2,192]{2,1,0:T(2,128)(2,1)S(1)}, u32[]{:S(2)}, u32[]{:S(2)}) async-start(bf16[16,2,192]{2,1,0:T(2,128)(2,1)} %reshape.117), calls=%async_computation.1 | async-start | bytes 32768 | tf_op jit(solution)/shard_map/all_to_all | solution.py:44
  26.8 111.0 %all-to-all-start = ((bf16[48,16,1024]{2,0,1:T(8,128)(2,1)}), bf16[48,16,1024]{2,0,1:T(8,128)(2,1)}, u32[]{:S(2)}, u32[]{:S(2)}) async-start(bf16[48,16,1024]{2,0,1:T(8,128)(2,1)} %bitcast.67), calls=%async_computation | async-start | bytes 3145728 | tf_op jit(solution)/shard_map/all_to_all | solution.py:43
  31.2 306.4 %reduce-scatter.2.cloned.1.call-start = ((), (), s32[]{:S(2)}) async-start(), calls=%async_computation.4 | async-start | bytes 8912896 | tf_op jit(solution)/shard_map/reduce_scatter | solution.py:52
  158.9 32.4 %copy-start = (bf16[6,128,4096]{2,1,0:T(8,128)(2,1)}, bf16[6,128,4096]{2,1,0:T(8,128)(2,1)S(1)}, u32[]{:S(2)}) copy-start(bf16[6,128,4096]{2,1,0:T(8,128)(2,1)S(1)} %divide_convert_fusion) | copy-start | bytes 18874372
Sparse Core Ops, SparseCore 0:
  9.1 119.8 all-gather.2
  231.9 105.6 reduce-scatter.1
where the time goes:
time: 345 us; the launch traced here: 344 us
  waiting for transfers between devices  112 us (32%)
  blocking collectives  82 us (24%)
  matrix products  72.7 us (21%)
  local copies, waits for them, and re-layouts  28.8 us (8%)
  other arithmetic  21.1 us (6%)
  starting transfers between devices  13.9 us (4%)
  between operations  13.5 us (4%)
    reduce_scatter x1, waiting for transfers between devices, shards(): lax.psum_scatter(group_product(grad_q, grad_scale, hidden_q, hidden_scale...  106 us
    all_gather x1, blocking collectives, shards(): lax.all_gather(dy_scales, 'tensor', axis=0, tiled=True)  82 us
    dot_general x6, matrix products, group_product(): lax.dot_general(grad_block, hidden_block, (((0,), (0,)), ((), ())), prefe...  72.7 us
    mul x4, local copies, waits for them, and re-layouts, dequantize(): widened = widened * scales.astype(jnp.float32)[:, :, None]  24.1 us
    reduce_max x2, other arithmetic, requantize(): largest = jnp.max(jnp.abs(blocked), axis=1)  11.1 us
    all_to_all x1, starting transfers between devices, shards(): lax.all_to_all(h_scales, 'tensor', split_axis=1, concat_axis=0, tiled=True)  9.5 us
    convert_element_type x2, other arithmetic, requantize(): (blocked / column_scale.astype(jnp.float32)[:, None, :]).astype(jnp.bfloa...  8.04 us
  transfers between devices with their start and end apart: 4, of which 2 were waited for; matrix products, arithmetic and copies ran while one was open for 10% of the time, Pallas kernels for 0%

commit v1 on v0

--- a/solution.py
+++ b/solution.py
@@ -4,6 +4,11 @@
 from jax.sharding import PartitionSpec as P
 
 QBLOCK = 128
+
+
+def gather_over(array, axis, along):
+    sent = jnp.stack([array] * lax.axis_size(axis))
+    return jnp.concatenate(lax.all_to_all(sent, axis, 0, 0), axis=along)
 
 
 def dequantize(values, scales):
@@ -45,7 +50,7 @@
     )
     grad_vals, grad_blocks = (
         lax.all_gather(dy_values, "tensor", axis=0, tiled=True),
-        lax.all_gather(dy_scales, "tensor", axis=0, tiled=True),
+        gather_over(dy_scales, "tensor", 0),
     )
     hidden_q, hidden_scale = requantize(dequantize(hidden_vals, hidden_blocks))
     grad_q, grad_scale = requantize(dequantize(grad_vals, grad_blocks))

time: 345 us -> 332 us (0.962)
  blocking collectives: 82 us -> 0 us
  waiting for transfers between devices: 112 us -> 178 us
  starting transfers between devices: 13.9 us -> 17.4 us
    all_gather x1 -> x0, blocking collectives: 82 us -> none  [shards(): lax.all_gather(dy_scales, 'tensor', axis=0, tiled=True)]
    all_to_all x1, waiting for transfers between devices: 0.01 us -> 29.7 us  [shards(): lax.all_to_all(h_values, 'tensor', split_axis=1, concat_axis=0, tiled=True)]
    all_gather x1, waiting for transfers between devices: 0.02 us -> 27.2 us  [shards(): lax.all_gather(dy_values, 'tensor', axis=0, tiled=True)]
    all_to_all x0 -> x1, waiting for transfers between devices: none -> 5.89 us  [gather_over(): return jnp.concatenate(lax.all_to_all(sent, axis, 0, 0), axis=along)]
    all_to_all x0 -> x1, starting transfers between devices: none -> 3.5 us  [gather_over(): return jnp.concatenate(lax.all_to_all(sent, axis, 0, 0), axis=along)]
  transfers between devices with their start and end apart: 4 -> 5, of which waited for: 2 -> 5; matrix products, arithmetic and copies ran while one was open for 10% -> 10% of each run, Pallas kernels for 0% -> 0%
where the time goes in v1:
time: 332 us
  waiting for transfers between devices  178 us (54%)
  matrix products  72.8 us (22%)
  local copies, waits for them, and re-layouts  30.8 us (9%)
  other arithmetic  19.2 us (6%)
  starting transfers between devices  17.4 us (5%)
  between operations  13.6 us (4%)
    reduce_scatter x1, waiting for transfers between devices, shards(): lax.psum_scatter(group_product(grad_q, grad_scale, hidden_q, hidden_scale...  107 us
    dot_general x6, matrix products, group_product(): lax.dot_general(grad_block, hidden_block, (((0,), (0,)), ((), ())), prefe...  72.8 us
    all_to_all x1, waiting for transfers between devices, shards(): lax.all_to_all(h_values, 'tensor', split_axis=1, concat_axis=0, tiled=True)  29.7 us
    all_gather x1, waiting for transfers between devices, shards(): lax.all_gather(dy_values, 'tensor', axis=0, tiled=True)  27.2 us
    mul x4, local copies, waits for them, and re-layouts, dequantize(): widened = widened * scales.astype(jnp.float32)[:, :, None]  24.2 us
    all_to_all x1, starting transfers between devices, shards(): lax.all_to_all(h_scales, 'tensor', split_axis=1, concat_axis=0, tiled=True)  9.5 us
    reduce_max x2, other arithmetic, requantize(): largest = jnp.max(jnp.abs(blocked), axis=1)  9.24 us
    convert_element_type x2, other arithmetic, requantize(): (blocked / column_scale.astype(jnp.float32)[:, None, :]).astype(jnp.bfloa...  8.04 us
  transfers between devices with their start and end apart: 5, of which 5 were waited for; matrix products, arithmetic and copies ran while one was open for 10% of the time, Pallas kernels for 0%

profile of v1, /device:TPU:8, one launch (start us, length us, event | category | flops | bytes accessed | tf_op | source)
XLA Modules:
  0.0 331.6 jit_solution(15474981177428751049)
XLA Ops:
  6.5 0.0 copy-start
  6.5 0.0 all-gather.2.cloned.1.call-start
  6.5 0.7 all-gather.2.cloned.1.call-update
  7.3 0.8 copy.22
  8.1 0.7 reshape.126
  8.8 9.5 %all-to-all-start.2 = ((bf16[16,2,192]{2,1,0:T(2,128)(2,1)}), bf16[16,2,192]{2,1,0:T(2,128)(2,1)S(1)}, u32[]{:S(2)}, u32[]{:S(2)}) async-start(bf16[16,2,192]{2,1,0:T(2,128)(2,1)} %reshape.126), calls=%async_computation.2 | async-start | bytes 32768 | tf_op jit(solution)/shard_map/all_to_all | solution.py:49
  18.3 0.0 copy-done
  18.3 0.8 reshape.124
  19.2 7.6 %all-to-all-done.2 = bf16[16,2,192]{2,1,0:T(2,128)(2,1)S(1)} async-done(((bf16[16,2,192]{2,1,0:T(2,128)(2,1)}), bf16[16,2,192]{2,1,0:T(2,128)(2,1)S(1)}, u32[]{:S(2)}, u32[]{:S(2)}) %all-to-all-start.2) | async-done | bytes 12320 | tf_op jit(solution)/shard_map/all_to_all | solution.py:49
  26.8 3.5 %all-to-all-start = ((bf16[16,2,768]{2,1,0:T(2,128)(2,1)}), bf16[16,2,768]{2,1,0:T(2,128)(2,1)S(1)}, u32[]{:S(2)}, u32[]{:S(2)}) async-start(bf16[16,2,768]{2,1,0:T(2,128)(2,1)} %reshape.124), calls=%async_computation | async-start | bytes 98304 | tf_op jit(solution)/shard_map/all_to_all | solution.py:11
  30.3 2.8 copy.31
  33.1 5.9 %all-to-all-done = bf16[16,2,768]{2,1,0:T(2,128)(2,1)S(1)} async-done(((bf16[16,2,768]{2,1,0:T(2,128)(2,1)}), bf16[16,2,768]{2,1,0:T(2,128)(2,1)S(1)}, u32[]{:S(2)}, u32[]{:S(2)}) %all-to-all-start) | async-done | bytes 49184 | tf_op jit(solution)/shard_map/all_to_all | solution.py:11
  39.0 0.0 copy-start.4
  39.0 4.4 %all-to-all-start.1 = ((bf16[48,16,1024]{2,0,1:T(8,128)(2,1)}), bf16[48,16,1024]{2,0,1:T(8,128)(2,1)}, u32[]{:S(2)}, u32[]{:S(2)}) async-start(bf16[48,16,1024]{2,0,1:T(8,128)(2,1)} %bitcast.69), calls=%async_computation.1 | async-start | bytes 3145728 | tf_op jit(solution)/shard_map/all_to_all | solution.py:48
  43.4 0.0 reduce-scatter.2.cloned.1.call-start
  43.4 0.0 copy-done.4
  43.5 0.1 reshape.127
  43.6 0.2 copy.26
  43.7 0.9 mul.151
  44.6 2.3 mul.152
  46.9 1.0 reshape.125
  47.9 0.1 copy.25
  48.0 7.0 %mul.148 = f32[768,32,128]{2,1,0:T(8,128)} broadcast(f32[768,32]{1,0:T(8,128)S(1)} %bitcast.73), dimensions={0,1} | broadcast | bytes 12681216 | tf_op jit(solution)/shard_map/mul | solution.py:18
  55.1 0.0 copy-start.3
  55.1 14.0 %mul.149 = f32[6,128,4096]{2,1,0:T(8,128)} reshape(f32[768,32,128]{2,1,0:T(8,128)} %mul.148) | data formatting | bytes 25165824 | tf_op jit(solution)/shard_map/mul | solution.py:18
  69.1 29.7 %all-to-all-done.1 = bf16[48,16,1024]{2,0,1:T(8,128)(2,1)} async-done(((bf16[48,16,1024]{2,0,1:T(8,128)(2,1)}), bf16[48,16,1024]{2,0,1:T(8,128)(2,1)}, u32[]{:S(2)}, u32[]{:S(2)}) %all-to-all-start.1) | async-done | bytes 1572896 | tf_op jit(solution)/shard_map/all_to_all | solution.py:48
  98.8 1.8 convert_element_type.180
  100.6 0.0 copy-done.3
  100.6 0.8 abs_reduce_fusion.1
  101.4 0.4 divide_convert_fusion.1
  101.9 27.2 %all-gather.2.cloned.1.call-done = bf16[768,4096]{1,0:T(8,128)(2,1)} async-done(((bf16[48,4096]{1,0:T(8,128)(2,1)}), bf16[768,4096]{1,0:T(8,128)(2,1)}) %all-gather.2.cloned.1.call-update) | async-done | bytes 6291472 | tf_op jit(solution)/shard_map/all_gather | solution.py:52
  129.1 8.5 %abs_reduce_fusion = f32[6,4096]{1,0:T(8,128)S(1)} fusion(f32[6,128,4096]{2,1,0:T(8,128)} %mul.149, bf16[6,128,4096]{2,1,0:T(8,128)(2,1)} %bitcast.70), kind=kLoop, calls=%fused_computation.3 | loop fusion | flops 12558336 | bytes 18972672 | tf_op jit(solution)/shard_map/reduce_max | solution.py:25
  137.7 7.6 %divide_convert_fusion = bf16[6,128,4096]{2,1,0:T(8,128)(2,1)S(1)} fusion(f32[6,128,4096]{2,1,0:T(8,128)} %mul.149, bf16[6,128,4096]{2,1,0:T(8,128)(2,1)} %bitcast.71, f32[6,4096]{1,0:T(8,128)S(1)} %get-tuple-element.9), kind=kLoop, calls=%fused_computation.2 | loop fusion | flops 12582912 | bytes 25264128 | tf_op jit(solution)/shard_map/convert_element_type | solution.py:27
  145.2 0.0 copy-start.2
  145.3 8.1 %fusion = f32[4096,1024]{1,0:T(8,128)} fusion(bf16[6,128,4096]{2,1,0:T(8,128)(2,1)S(1)} %divide_convert_fusion, bf16[6,128,1024]{2,1,0:T(8,128)(2,1)S(1)} %divide_convert_fusion.1), kind=kOutput, calls=%fused_computation.9 | convolution fusion | flops 1073741824 | bytes 18087936 | tf_op jit(solution)/shard_map/dot_general | solution.py:37
  153.4 8.1 %fusion.1 = f32[4096,1024]{1,0:T(8,128)} fusion(bf16[6,128,4096]{2,1,0:T(8,128)(2,1)S(1)} %divide_convert_fusion, bf16[6,128,1024]{2,1,0:T(8,128)(2,1)S(1)} %divide_convert_fusion.1), kind=kOutput, calls=%fused_computation.11 | convolution fusion | flops 1073741824 | bytes 18087936 | tf_op jit(solution)/shard_map/dot_general | solution.py:37
  161.5 8.1 %fusion.2 = f32[4096,1024]{1,0:T(8,128)} fusion(bf16[6,128,4096]{2,1,0:T(8,128)(2,1)S(1)} %divide_convert_fusion, bf16[6,128,1024]{2,1,0:T(8,128)(2,1)S(1)} %divide_convert_fusion.1), kind=kOutput, calls=%fused_computation.13 | convolution fusion | flops 1073741824 | bytes 18087936 | tf_op jit(solution)/shard_map/dot_general | solution.py:37
  169.6 8.1 %fusion.3 = f32[4096,1024]{1,0:T(8,128)} fusion(bf16[6,128,4096]{2,1,0:T(8,128)(2,1)S(1)} %divide_convert_fusion, bf16[6,128,1024]{2,1,0:T(8,128)(2,1)S(1)} %divide_convert_fusion.1), kind=kOutput, calls=%fused_computation.15 | convolution fusion | flops 1073741824 | bytes 18087936 | tf_op jit(solution)/shard_map/dot_general | solution.py:37
  177.7 0.0 copy-done.2
  177.7 8.2 %fusion.4 = f32[4096,1024]{1,0:T(8,128)} fusion(bf16[6,128,4096]{2,1,0:T(8,128)(2,1)S(1)} %divide_convert_fusion, bf16[6,128,1024]{2,1,0:T(8,128)(2,1)S(1)} %divide_convert_fusion.1), kind=kOutput, calls=%fused_computation.17 | convolution fusion | flops 1073741824 | bytes 18087936 | tf_op jit(solution)/shard_map/dot_general | solution.py:37
  185.8 0.1 slice_convert_fusion.5
  185.9 0.0 copy-start.1
  185.9 32.2 %add_convert_fusion = bf16[4096,1024]{1,0:T(8,128)(2,1)} fusion(f32[4096,1024]{1,0:T(8,128)} %fusion, f32[4096,1024]{1,0:T(8,128)} %fusion.1, f32[4096,1024]{1,0:T(8,128)} %fusion.2, f32[4096,1024]{1,0:T(8,128)} %fusion.3, f32[4096,1024]{1,0:T(8,128)} %fusion.4, f32[1024]{0:T(1024)S(1)} %bitcast.88, f32[4096]{0:T(1024)S(1)} %bitcast.82, ...), kind=kOutput, calls=%fused_computation | convolution fusion | flops 1149239296 | bytes 93708288 | tf_op jit(solution)/shard_map/dot_general | solution.py:37
  218.2 0.0 reduce-scatter.2.cloned.1.call-update
  218.2 106.6 %reduce-scatter.2.cloned.1.call-done = bf16[256,1024]{1,0:T(8,128)(2,1)} async-done(((bf16[4096,1024]{1,0:T(8,128)(2,1)}), bf16[256,1024]{1,0:T(8,128)(2,1)}) %reduce-scatter.2.cloned.1.call-update) | async-done | bytes 524304 | tf_op jit(solution)/shard_map/reduce_scatter | solution.py:57
  324.8 0.0 copy-done.1
  (6 shorter events, 0.1 us)
Async XLA Ops:
  6.5 11.8 %copy-start = (bf16[48,32]{0,1:T(8,128)(2,1)S(1)}, bf16[48,32]{0,1:T(8,128)(2,1)}, u32[]{:S(2)}) copy-start(bf16[48,32]{0,1:T(8,128)(2,1)} %param.7) | copy-start | bytes 9220
  6.5 122.6 %all-gather.2.cloned.1.call-start = ((), (), s32[]{:S(2)}) async-start(), calls=%async_computation.4 | async-start | bytes 6684672 | tf_op jit(solution)/shard_map/all_gather | solution.py:52
  8.8 18.0 %all-to-all-start.2 = ((bf16[16,2,192]{2,1,0:T(2,128)(2,1)}), bf16[16,2,192]{2,1,0:T(2,128)(2,1)S(1)}, u32[]{:S(2)}, u32[]{:S(2)}) async-start(bf16[16,2,192]{2,1,0:T(2,128)(2,1)} %reshape.126), calls=%async_computation.2 | async-start | bytes 32768 | tf_op jit(solution)/shard_map/all_to_all | solution.py:49
  26.8 12.2 %all-to-all-start = ((bf16[16,2,768]{2,1,0:T(2,128)(2,1)}), bf16[16,2,768]{2,1,0:T(2,128)(2,1)S(1)}, u32[]{:S(2)}, u32[]{:S(2)}) async-start(bf16[16,2,768]{2,1,0:T(2,128)(2,1)} %reshape.124), calls=%async_computation | async-start | bytes 98304 | tf_op jit(solution)/shard_map/all_to_all | solution.py:11
  39.0 4.5 %copy-start.4 = (bf16[16,2,768]{2,1,0:T(2,128)(2,1)}, bf16[16,2,768]{2,1,0:T(2,128)(2,1)S(1)}, u32[]{:S(2)}) copy-start(bf16[16,2,768]{2,1,0:T(2,128)(2,1)S(1)} %all-to-all-done) | copy-start | bytes 147460
  39.0 59.8 %all-to-all-start.1 = ((bf16[48,16,1024]{2,0,1:T(8,128)(2,1)}), bf16[48,16,1024]{2,0,1:T(8,128)(2,1)}, u32[]{:S(2)}, u32[]{:S(2)}) async-start(bf16[48,16,1024]{2,0,1:T(8,128)(2,1)} %bitcast.69), calls=%async_computation.1 | async-start | bytes 3145728 | tf_op jit(solution)/shard_map/all_to_all | solution.py:48
  43.4 281.4 %reduce-scatter.2.cloned.1.call-start = ((), (), s32[]{:S(2)}) async-start(), calls=%async_computation.5 | async-start | bytes 8912896 | tf_op jit(solution)/shard_map/reduce_scatter | solution.py:57
  55.1 45.5 %copy-start.3 = (f32[6,128,1024]{2,1,0:T(8,128)S(1)}, f32[6,128,1024]{2,1,0:T(8,128)}, u32[]{:S(2)}) copy-start(f32[6,128,1024]{2,1,0:T(8,128)} %mul.152) | copy-start | bytes 9437188
  145.2 32.4 %copy-start.2 = (bf16[6,128,4096]{2,1,0:T(8,128)(2,1)}, bf16[6,128,4096]{2,1,0:T(8,128)(2,1)S(1)}, u32[]{:S(2)}) copy-start(bf16[6,128,4096]{2,1,0:T(8,128)(2,1)S(1)} %divide_convert_fusion) | copy-start | bytes 18874372
  185.9 138.9 %copy-start.1 = (bf16[48,32]{0,1:T(8,128)(2,1)S(1)}, bf16[48,32]{0,1:T(8,128)(2,1)}, u32[]{:S(2)}) copy-start(bf16[48,32]{0,1:T(8,128)(2,1)} %param.7) | copy-start | bytes 9220
Sparse Core Ops, SparseCore 0:
  9.1 119.9 all-gather.1
  218.3 106.4 reduce-scatter.1
